TPU v7x, 128 devices: a whole 4x4x4 slice. The times are simulated.
128 devices in a mesh: space: 16 (over z_lo, y, core), mode: 8 (over x, z_hi).
Axes of the slice: x: 4, y: 4, z: 4 (z_hi: 2, z_lo: 2; z = z_hi * 2 + z_lo), core: 2. Of those that a mesh axis runs over, the one named last changes fastest.
Arguments:
- test_modes: float32 [32, 3, 8, 32, 256], P(None, None, None, 'space'), may hold values from -6 to 6
- modes: float32 [128, 3, 8, 32, 256], P('mode', None, None, 'space'), may hold values from -6 to 6
Outputs:
- triad: float32 [32, 128, 128], P('space', 'mode')
All inputs are finite; a program needn't handle non-finite values.
Results may differ from a plain program's by a relative error of at most 0.000071.
Values sent between devices are 32-bit elements; how exact they have to be, the bound alone decides.
A program may use at most 64 MiB of HBM per device.

v0:
```python
import math

import jax
import jax.numpy as jnp
from jax import lax
from jax.sharding import PartitionSpec as P

MODES = 128
NX = 256
NZ = 8
BLOCK = 2048


def extended(value, sides, width):
    for axis, dim in sides:
        size, length = (lax.axis_size(axis), value.shape[dim])
        up = [(i, (i + 1) % size) for i in range(size)]
        down = [(j, i) for i, j in up]
        last = lax.slice_in_dim(value, length - width, length, axis=dim)
        leading = lax.slice_in_dim(value, 0, width, axis=dim)
        before = lax.ppermute(last, axis, up)
        after = lax.ppermute(leading, axis, down)
        value = jnp.concatenate([before, value, after], axis=dim)
    return value


def in_blocks(value, dim, size):
    shape = value.shape
    parts = value.reshape(*shape[:dim], size, shape[dim] // size, *shape[dim + 1 :])
    return jnp.moveaxis(parts, dim, 0)


def sent_and_summed(value, axis, dim):
    parts = in_blocks(value, dim, lax.axis_size(axis))
    arrived = lax.all_to_all(parts, axis, split_axis=0, concat_axis=0, tiled=True)
    return arrived.sum(axis=0)


def central_diff(field, along):
    ahead = jnp.roll(field, -1, along) - jnp.roll(field, 1, along)
    farther = jnp.roll(field, -2, along) - jnp.roll(field, 2, along)
    return (8.0 * ahead - farther) / 12.0


def per_device(test_modes, modes):
    local_count = modes.shape[0]
    test_count = test_modes.shape[0]
    row_count = modes.shape[3]
    padded = extended(modes, (("space", 3),), 2)
    ahead = padded[:, :, :, 3 : row_count + 3] - padded[:, :, :, 1 : row_count + 1]
    farther = padded[:, :, :, 4 : row_count + 4] - padded[:, :, :, 0:row_count]
    along_y = (8.0 * ahead - farther) / 12.0
    gradients = jnp.stack([central_diff(modes, 4), along_y, central_diff(modes, 2)], axis=2)
    gradients = gradients.reshape(local_count, 3, 3, -1)
    test_flat = test_modes.reshape(test_count, 3, -1)
    mode_flat = modes.reshape(local_count, 3, -1)
    cell_count = test_flat.shape[2]
    block_count = cell_count // BLOCK
    volume_scale = 1.0 / math.sqrt(NX * NZ * row_count * lax.axis_size("space"))

    def weigh(offset):
        test_block = lax.dynamic_slice_in_dim(test_flat, offset, BLOCK, 2)
        grad_block = lax.dynamic_slice_in_dim(gradients, offset, BLOCK, 3)
        weighted = test_block[:, 0, None, None, :] * grad_block[None, :, 0]
        weighted = weighted + test_block[:, 1, None, None, :] * grad_block[None, :, 1]
        weighted = weighted + test_block[:, 2, None, None, :] * grad_block[None, :, 2]
        return weighted

    def add_piece(running, weighted, piece_block):
        partial_value = jnp.einsum(
            "ikbc,jbc->ikj", weighted, piece_block, precision=lax.Precision.HIGHEST
        )
        return running + partial_value

    initial = jnp.zeros((test_count, local_count, MODES), jnp.float32)
    everything = lax.all_gather(mode_flat, "mode", axis=0, tiled=True)

    def one_block(index_block, running):
        offset = index_block * BLOCK
        weighted = weigh(offset)
        piece_block = lax.dynamic_slice_in_dim(everything, offset, BLOCK, 2)
        return add_piece(running, weighted, piece_block)

    partial_triad = lax.fori_loop(0, block_count, one_block, initial)
    partial_triad = partial_triad * volume_scale
    result = sent_and_summed(partial_triad, "space", 0)
    return result


def solution(mesh):
    in_specs = (P(None, None, None, "space", None), P("mode", None, None, "space", None))
    out_specs = P("space", "mode", None)
    return jax.shard_map(
        per_device, mesh=mesh, in_specs=in_specs, out_specs=out_specs, check_vma=False
    )
```

profile of v0, /device:TPU:0, one launch (start us, length us, event | category | flops | bytes accessed | tf_op | source)
XLA Modules:
  0.0 155.1 jit_solution(17726550223214487848)
XLA Ops:
  6.5 1.5 copy.22
  8.1 1.6 %reshape.137 = f32[16,3,4096]{2,0,1:T(8,128)} reshape(f32[16,3,8,2,256]{4,3,2,0,1:T(2,128)S(1)} %copy.22) | data formatting | bytes 1572864 | tf_op jit(solution)/shard_map/reshape | solution.py:56
  9.7 4.0 %collective-permute-start = (f32[16,3,8,2,256]{4,3,2,1,0:T(2,128)}, f32[16,3,8,2,256]{4,3,2,1,0:T(2,128)}, u32[]{:S(2)}, u32[]{:S(2)}) collective-permute-start(f32[16,3,8,2,256]{4,3,2,1,0:T(2,128)} %param.5), channel_id=1, source_target_pairs={{8,0},{16,8},{24,16},{32,24},{40,32},{48,40},{56,48},{64,56},{72,6... | collective-permute-start | bytes 2359304 | tf_op jit(solution)/shard_map/ppermute | solution.py:22
  13.7 1.6 %fusion.35 = (f32[16,3,8,2,1]{4,3,2,1,0:T(2,128)S(1)}, f32[16,3,8,2,1]{4,3,2,1,0:T(2,128)S(1)}) fusion(f32[16,3,8,2,256]{4,3,2,1,0:T(2,128)} %param.5), kind=kLoop, calls=%fused_computation.55 | loop fusion | bytes 12288 | tf_op jit(solution)/shard_map/jit(_roll_static)/slice | solution.py:40
  15.3 0.4 copy.24
  15.6 0.4 copy.14
  16.1 0.4 copy.25
  16.4 0.4 copy.16
  16.9 0.5 slice_bitcast_fusion.8
  17.4 1.1 slice_bitcast_fusion
  18.5 1.1 slice_bitcast_fusion.2
  19.6 3.2 %fusion.30 = f32[16,3,1,8,2,256]{5,4,3,1,0,2:T(2,128)S(1)} fusion(f32[16,3,1,8,2,1]{5,4,3,1,0,2:T(2,128)S(1)} %copy.14, f32[16,3,1,8,2,255]{5,4,3,1,0,2:T(2,128)S(1)} %get-tuple-element.141, f32[16,3,1,8,2,255]{5,4,3,1,0,2:T(2,128)S(1)} %get-tuple-element.140, f32[16,3,1,8,2,1]{5,4,3,1,0,2:T(2,128)S(1)} %copy.16, ...), kind=kLoop, calls=%fused_computation.32 | loop fusion | flops 1769472 | bytes 3932160 | tf_op jit(solution)/shard_map/div | solution.py:42
  23.1 0.6 div.14
  23.9 0.3 slice_bitcast_fusion.6
  24.3 0.4 slice_bitcast_fusion.4
  24.6 1.3 fusion.33
  26.3 1.6 %div.17 = f32[16,3,1,4096]{3,0,2,1:T(8,128)} reshape(f32[16,3,1,8,2,256]{5,4,3,0,1,2:T(2,128)S(1)} %copy.21) | data formatting | bytes 1572864 | tf_op jit(solution)/shard_map/div | solution.py:42
  27.9 2.1 %copy.12 = f32[32,3,8,2,256]{4,3,2,0,1:T(2,128)S(1)} copy(f32[32,3,8,2,256]{4,3,2,1,0:T(2,128)} %param.4) | data formatting | bytes 3145728 | tf_op args[0]
  30.1 2.4 %reshape.136 = f32[32,3,4096]{2,0,1:T(8,128)} reshape(f32[32,3,8,2,256]{4,3,2,0,1:T(2,128)S(1)} %copy.12) | data formatting | bytes 3145728 | tf_op jit(solution)/shard_map/reshape | solution.py:55
  32.5 3.9 %fusion.34 = f32[16,3,8,2,256]{4,3,2,1,0:T(2,128)S(1)} fusion(f32[16,3,8,2,256]{4,3,2,1,0:T(2,128)} %collective-permute-done, f32[16,3,8,2,256]{4,3,2,1,0:T(2,128)} %collective-permute-done.1, f32[16,3,8,2,256]{4,3,2,1,0:T(2,128)S(1)} %copy-done), kind=kLoop, calls=%fused_computation.43 | loop fusion | flops 1376256 | bytes 3145728 | tf_op jit(solution)/shard_map/div | solution.py:52
  36.4 0.3 copy.18
  36.7 1.5 stack.8
  38.3 1.6 %pad_maximum_fusion = f32[16,3,3,4096]{3,0,2,1:T(8,128)S(1)} fusion(f32[16,3,1,4096]{3,0,2,1:T(8,128)} %div.17, f32[16,3,1,4096]{3,0,2,1:T(8,128)} %stack.8, f32[16,3,1,4096]{3,0,2,1:T(8,128)S(1)} %div.14), kind=kLoop, calls=%fused_computation.23 | loop fusion | flops 1179648 | bytes 4718592 | tf_op jit(solution)/shard_map/stack | solution.py:53
  39.9 61.6 %all-gather.2.cloned.1.call-done = f32[128,3,4096]{2,0,1:T(8,128)} async-done(((f32[16,3,4096]{2,0,1:T(8,128)}), f32[128,3,4096]{2,0,1:T(8,128)}) %all-gather.2.cloned.1.call-update) | async-done | bytes 6291472 | tf_op jit(solution)/shard_map/all_gather | solution.py:76
  101.5 33.1 %while.14 = (s32[]{:T(128)}, f32[32,16,128]{2,1,0:T(8,128)}, f32[32,3,4096]{2,0,1:T(8,128)}, f32[16,3,3,4096]{3,0,2,1:T(8,128)S(1)}, f32[128,3,4096]{2,0,1:T(8,1...) while((s32[]{:T(128)}, f32[32,16,128]{2,1,0:T(8,128)}, ...), condition=%wide.region_1.2_spmd.clone, body=%wide.region_0.1_spmd.clone.sunk | while | flops 4847697920 | bytes 9568473 | solution.py:84
  101.6 2.1 %dynamic-slice_bitcast_fusion.9 = (f32[32,2048]{1,0:T(8,128)}, f32[32,2048]{1,0:T(8,128)}, f32[32,2048]{1,0:T(8,128)}) fusion(f32[32,3,4096]{2,0,1:T(8,128)} %get-tuple-element.217, s32[]{:T(128)S(6)} %select_n.11, s32[]{:T(128)S(6)} %add.82, s32[]{:T(128)S(6)} %add.83), kind=kLoop, calls=%fused_computation.21.clone.1 | loop fusion | bytes 1572876 | tf_op jit(solution)/shard_map/while/body/eval_jaxpr/mul | solution.py:64
  103.7 14.3 %fusion.41 = f32[32,16,128]{2,1,0:T(8,128)} fusion(f32[128,3,4096]{2,0,1:T(8,128)} %get-tuple-element.219, s32[]{:T(128)S(6)} %select_n.11, f32[16,3,2048]{2,0,1:T(8,128)S(1)} %get-tuple-element.187, f32[32,2048]{1,0:T(8,128)} %get-tuple-element.188, f32[16,3,2048]{2,0,1:T(8,128)S(1)} %get-tuple-element.189, f32[32,2048]{1,0:T(8,128)} %get-tuple-element.190, ...), kind=kOutput, calls=%fused_computation.15.clone.1 | convolution fusion | flops 4847697920 | bytes 5636101 | tf_op jit(solution)/shard_map/while/body/eval_jaxpr/ikbc,jbc->ikj/dot_general | solution.py:70
  118.2 2.1 %dynamic-slice_bitcast_fusion.9 = (f32[32,2048]{1,0:T(8,128)}, f32[32,2048]{1,0:T(8,128)}, f32[32,2048]{1,0:T(8,128)}) fusion(f32[32,3,4096]{2,0,1:T(8,128)} %get-tuple-element.217, s32[]{:T(128)S(6)} %select_n.11, s32[]{:T(128)S(6)} %add.82, s32[]{:T(128)S(6)} %add.83), kind=kLoop, calls=%fused_computation.21.clone.1 | loop fusion | bytes 1572876 | tf_op jit(solution)/shard_map/while/body/eval_jaxpr/mul | solution.py:64
  120.3 14.3 %fusion.41 = f32[32,16,128]{2,1,0:T(8,128)} fusion(f32[128,3,4096]{2,0,1:T(8,128)} %get-tuple-element.219, s32[]{:T(128)S(6)} %select_n.11, f32[16,3,2048]{2,0,1:T(8,128)S(1)} %get-tuple-element.187, f32[32,2048]{1,0:T(8,128)} %get-tuple-element.188, f32[16,3,2048]{2,0,1:T(8,128)S(1)} %get-tuple-element.189, f32[32,2048]{1,0:T(8,128)} %get-tuple-element.190, ...), kind=kOutput, calls=%fused_computation.15.clone.1 | convolution fusion | flops 4847697920 | bytes 5636101 | tf_op jit(solution)/shard_map/while/body/eval_jaxpr/ikbc,jbc->ikj/dot_general | solution.py:70
  134.6 1.0 broadcast_multiply_fusion
  135.5 12.1 %all_to_all.5 = f32[16,2,16,128]{3,2,1,0:T(8,128)S(1)} all-to-all(f32[16,2,16,128]{3,2,1,0:T(8,128)S(1)} %bitcast.77), channel_id=1, replica_groups=mesh['space'=16,'mode'=8] {'space'}, dimensions={0} | all-to-all | bytes 524288 | tf_op jit(solution)/shard_map/all_to_all | solution.py:35
  147.7 0.6 reduce_sum.9
  (14 shorter events, 1.0 us)
Async XLA Ops:
  6.5 10.3 %copy-start = (f32[16,3,8,2,256]{4,3,2,1,0:T(2,128)S(1)}, f32[16,3,8,2,256]{4,3,2,1,0:T(2,128)}, u32[]{:S(2)}) copy-start(f32[16,3,8,2,256]{4,3,2,1,0:T(2,128)} %param.5) | copy-start | bytes 2359300
  6.5 95.0 %all-gather.2.cloned.1.call-start = ((), (), s32[]{:S(2)}) async-start(), calls=%async_computation.1 | async-start | bytes 7077888 | tf_op jit(solution)/shard_map/all_gather | solution.py:76
  9.7 22.8 %collective-permute-start = (f32[16,3,8,2,256]{4,3,2,1,0:T(2,128)}, f32[16,3,8,2,256]{4,3,2,1,0:T(2,128)}, u32[]{:S(2)}, u32[]{:S(2)}) collective-permute-start(f32[16,3,8,2,256]{4,3,2,1,0:T(2,128)} %param.5), channel_id=1, source_target_pairs={{8,0},{16,8},{24,16},{32,24},{40,32},{48,40},{56,48},{64,56},{72,6... | collective-permute-start | bytes 2359304 | tf_op jit(solution)/shard_map/ppermute | solution.py:22
  13.7 18.8 %collective-permute-start.1 = (f32[16,3,8,2,256]{4,3,2,1,0:T(2,128)}, f32[16,3,8,2,256]{4,3,2,1,0:T(2,128)}, u32[]{:S(2)}, u32[]{:S(2)}) collective-permute-start(f32[16,3,8,2,256]{4,3,2,1,0:T(2,128)} %param.5), channel_id=1, source_target_pairs={{0,8},{8,16},{16,24},{24,32},{32,40},{40,48},{48,56},{56,64},{64,7... | collective-permute-start | bytes 2359304 | tf_op jit(solution)/shard_map/ppermute | solution.py:21
Sparse Core Ops, SparseCore 0:
  9.8 91.6 all-gather.1
where the time goes:
time: 156 us; the launch traced here: 155 us
  waiting for transfers between devices  61.7 us (40%)
  matrix products  28.6 us (18%)
  local copies, waits for them, and re-layouts  23.5 us (15%)
  between operations  13.5 us (9%)
  blocking collectives  12.1 us (8%)
  other arithmetic  11.7 us (8%)
  starting transfers between devices  3.99 us (3%)
    all_gather x1, waiting for transfers between devices, per_device(): everything = lax.all_gather(mode_flat, 'mode', axis=0, tiled=True)  61.6 us
    dot_general x2, matrix products, add_piece(): jnp.einsum('ikbc,jbc->ikj', weighted, piece_block, precision=lax.Precisio...  28.6 us
    all_to_all x1, blocking collectives, sent_and_summed(): lax.all_to_all(parts, axis, split_axis=0, concat_axis=0, tiled=True)  12.1 us
    div x2, other arithmetic, central_diff(): return (8.0 * ahead - farther) / 12.0  4.57 us
    mul x4, local copies, waits for them, and re-layouts, weigh(): weighted = test_block[:, 0, None, None, :] * grad_block[None, :, 0]  4.42 us
    unnamed x6, local copies, waits for them, and re-layouts  4.38 us
    ppermute x1, starting transfers between devices, extended(): after = lax.ppermute(leading, axis, down)  3.99 us
    div x1, other arithmetic, per_device(): along_y = (8.0 * ahead - farther) / 12.0  3.94 us
  transfers between devices with their start and end apart: 3, of which 1 were waited for; matrix products, arithmetic and copies ran while one was open for 17% of the time, Pallas kernels for 0%

commit v1 on v0

v1 whole, which is shorter than its diff:
```python
import functools

import jax
import jax.numpy as jnp
from jax import lax
from jax.experimental import pallas as pl
from jax.experimental.pallas import tpu as pltpu
from jax.sharding import PartitionSpec as P

F32 = jnp.float32
BF16 = jnp.bfloat16
MESH = pl.DeviceIdType.MESH
SCALE = 1.0 / 12.0 / 256.0
TILES = 14
ORDERS = ((0, 1, 2), (1, 2, 0), (2, 0, 1), (0, 2, 1))


def kernel(test_hbm, mode_hbm, out_ref, x_modes, x_tests, sent, got, up, down, tests, grads,
           rhs, part, paired, land1, sum1, land2, sum2, land3, load_sem, a2a_send, a2a_recv,
           up_send, down_send, up_recv, down_recv, pair_send, pair_recv, red_send, red_recv):
    s = lax.axis_index("space")
    m = lax.axis_index("mode")
    core = s % 2
    cy = (s // 2) % 4
    zlo = s // 8
    cx = m // 2
    cz = (m % 2) * 2 + zlo
    place = (cx, cy, cz)

    def device(x, y, z, c):
        return ((z % 2) * 8 + y * 2 + c, x * 2 + z // 2)

    def shifted(axis, step):
        there = list(place)
        there[axis] = (there[axis] + step) % 4
        return device(*there, core)

    load_modes = pltpu.make_async_copy(mode_hbm, x_modes, load_sem.at[0])
    load_tests = pltpu.make_async_copy(test_hbm, x_tests, load_sem.at[1])
    load_modes.start()
    load_tests.start()

    barrier = pltpu.get_barrier_semaphore()
    above = (s + 1) % 16
    below = (s + 15) % 16
    friends = [(s, (m + p) % 8) for p in range(1, 8)]
    friends += [(above, m), (below, m)]
    friends += [shifted(1, p) for p in range(1, 4)]
    friends += [shifted(2, p) for p in (1, 3)]
    for friend in friends:
        pl.semaphore_signal(barrier, inc=1, device_id=friend, device_id_type=MESH)

    lane = lax.broadcasted_iota(jnp.int32, (8, 128), 1)
    within = lane % 32
    low_half = lane < 64
    even_group = (lane // 32) % 2 == 0

    load_modes.wait()

    def arrange(at, carry):
        row = (at // 4) * 32 + (at % 4) * 4
        for xt in range(2):
            for kh in range(2):
                rows = [
                    x_modes[pl.ds(row + kh * 768 + (g // 2) * 16 + xt * 2 + g % 2, 8, stride=96), :]
                    for g in range(4)
                ]
                halves = []
                for g in range(2):
                    halves.append(jnp.where(low_half, rows[g], pltpu.roll(rows[g + 2], 64, 1)))
                for g in range(2):
                    halves.append(jnp.where(low_half, pltpu.roll(rows[g], 64, 1), rows[g + 2]))
                for c in range(2):
                    b0, b1 = halves[2 * c], halves[2 * c + 1]
                    first = jnp.where(even_group, b0, pltpu.roll(b1, 32, 1))
                    second = jnp.where(even_group, pltpu.roll(b0, 96, 1), b1)
                    sent[xt * 4 + 2 * c, at, pl.ds(kh * 8, 8), :] = first
                    sent[xt * 4 + 2 * c + 1, at, pl.ds(kh * 8, 8), :] = second
        return carry

    lax.fori_loop(0, 12, arrange, 0)

    def edges(d, carry):
        left, right = (d + 7) % 8, (d + 1) % 8
        for kh in range(2):
            rows = pl.ds(kh * 8, 8)
            for pack in range(2):
                packed = jnp.zeros((8, 128), F32)
                for slot in range(8 if pack == 0 else 4):
                    at = pack * 8 + slot
                    turn = 4 * slot - 30
                    from_left = pltpu.roll(sent[left, at, rows, :], (turn - 32) % 128, 1)
                    from_right = pltpu.roll(sent[right, at, rows, :], (turn + 32) % 128, 1)
                    spot = within - 4 * slot
                    packed = jnp.where((spot == 0) | (spot == 1), from_left, packed)
                    packed = jnp.where((spot == 2) | (spot == 3), from_right, packed)
                sent[d, 12 + pack, rows, :] = packed
        return carry

    lax.fori_loop(0, 8, edges, 0)

    pl.semaphore_wait(barrier, len(friends))

    def to_peer(p):
        return pltpu.make_async_remote_copy(
            src_ref=sent.at[(m + p) % 8], dst_ref=got.at[m],
            send_sem=a2a_send.at[p - 1], recv_sem=a2a_recv.at[p - 1],
            device_id=(s, (m + p) % 8), device_id_type=MESH)

    def to_above(p, src):
        k = (m + 8 - p) % 8
        return pltpu.make_async_remote_copy(
            src_ref=src, dst_ref=down.at[k], send_sem=up_send.at[p], recv_sem=down_recv.at[p],
            device_id=(above, m), device_id_type=MESH)

    def to_below(p, src):
        k = (m + 8 - p) % 8
        return pltpu.make_async_remote_copy(
            src_ref=src, dst_ref=up.at[k], send_sem=down_send.at[p], recv_sem=up_recv.at[p],
            device_id=(below, m), device_id_type=MESH)

    def start_peer(p, carry):
        to_peer(p).start()
        return carry

    lax.fori_loop(1, 8, start_peer, 0)
    own = sent.at[m, pl.ds(0, 12)]
    to_above(0, own).start()
    to_below(0, own).start()

    load_tests.wait()
    xt_mine, c_mine = m // 4, m % 4

    def arrange_tests(at, carry):
        row = (at // 4) * 32 + (at % 4) * 4 + xt_mine * 2
        for ih in range(4):
            value = None
            for g in range(4):
                line = x_tests[pl.ds(row + ih * 768 + (g // 2) * 16 + g % 2, 8, stride=96), :]
                line = pltpu.roll(line, (32 * g - 32 * c_mine + 128) % 128, 1)
                value = line if value is None else jnp.where(lane // 32 == g, line, value)
            tests[at, pl.ds(ih * 8, 8), :] = value
        return carry

    lax.fori_loop(0, 12, arrange_tests, 0)

    def split(value):
        high = value.astype(BF16)
        return high, (value - high.astype(F32)).astype(BF16)

    lane16 = lax.broadcasted_iota(jnp.int32, (16, 128), 1)
    in16 = lane16 % 32

    def first_grads(k):
        rows = pl.ds(pl.multiple_of(k * 16, 16), 16)
        for a in range(3):
            packed = got[k, 12 + a // 2]
            field = [got[k, a * 4 + t] for t in range(4)]
            turned = [pltpu.roll(f, 64, 1) for f in field]
            for t in range(4):
                f = field[t]
                slot = (a % 2) * 4 + t
                turn = 30 - 4 * slot

                def at_edge(step, edge):
                    moved = pltpu.roll(f, step % 128, 1)
                    halo = pltpu.roll(packed, (turn + step) % 128, 1)
                    return jnp.where(edge, halo, moved)

                near = at_edge(-1, in16 == 31) - at_edge(1, in16 == 0)
                far = at_edge(-2, in16 >= 30) - at_edge(2, in16 <= 1)
                grads[0, a, t, rows, :] = (8.0 * near - far) * SCALE

                def along_z(step):
                    n = t + step
                    return field[n] if 0 <= n < 4 else turned[n % 4]

                near = along_z(1) - along_z(-1)
                far = along_z(2) - along_z(-2)
                grads[2, a, t, rows, :] = (8.0 * near - far) * SCALE

    even16 = (lane16 // 32) % 2 == 0

    def second_grads(k):
        rows = pl.ds(pl.multiple_of(k * 16, 16), 16)
        for a in range(3):
            for t in range(4):
                here, over, under = got[k, a * 4 + t], up[k, a * 4 + t], down[k, a * 4 + t]
                before = pltpu.roll(here - under, 96, 1)
                after = pltpu.roll(over - here, 32, 1)
                near = jnp.where(even16, before, after)
                grads[1, a, t, rows, :] = (8.0 * near + (under - over)) * SCALE

    got[m] = sent[m]
    first_grads(m)

    def arrival(p, carry):
        k = (m + 8 - p) % 8
        to_peer(p).wait_recv()
        block = got.at[k, pl.ds(0, 12)]
        to_above(p, block).start()
        to_below(p, block).start()
        first_grads(k)
        return carry

    lax.fori_loop(1, 8, arrival, 0)

    def turn_modes(at, carry):
        field = got[:, at].reshape(128, 128).T
        high, low = split(field)
        rows = pl.ds(pl.multiple_of(at * 128, 128), 128)
        rhs[rows, 0:128] = high
        rhs[rows, 128:256] = low
        return carry

    lax.fori_loop(0, 12, turn_modes, 0)

    def triad_of(n, components):
        c = jnp.where(n < 8, 1 - core, core)
        y, zl = (n // 2) % 4, n % 2
        pair = zl * 8 + y * 2 + c
        total = None
        for b in components:
            for tp in range(2):
                columns = []
                for t in (2 * tp, 2 * tp + 1):
                    blocks = []
                    for r in range(2):
                        value = None
                        for a in range(3):
                            line = tests[a * 4 + t, pl.ds(pair * 2 + r, 1), :]
                            term = line * grads[b, a, t]
                            value = term if value is None else value + term
                        blocks.append(value)
                    columns.append(jnp.concatenate(blocks, axis=0))
                high, low = split(jnp.concatenate(columns, axis=1))
                left = jnp.concatenate([high, low], axis=0)
                right = rhs[(b * 4 + 2 * tp) * 128 : (b * 4 + 2 * tp + 2) * 128, :]
                piece = jnp.dot(left, right, preferred_element_type=F32)
                total = piece if total is None else total + piece
        value = (total[:256, :128] + total[:256, 128:]) + (total[256:, :128] + total[256:, 128:])
        return c, y, zl, value

    def spots(c, y, zl, x, zh, q):
        where = (x, y, zh * 2 + zl)
        first, second, third = ORDERS[q]
        return q, c, where[first], where[second], where[third]

    def phase1(n, carry):
        c, y, zl, value = triad_of(n, (0, 2))
        for r in range(2):
            for v in range(16):
                spot = spots(c, y, zl, v // 4, (v // 2) % 2, r * 2 + v % 2)
                part[spot] = value[r * 128 + v * 8 : r * 128 + v * 8 + 8]
        return carry

    def phase2(n, carry):
        c, y, zl, value = triad_of(n, (1,))
        for r in range(2):
            for v in range(16):
                spot = spots(c, y, zl, v // 4, (v // 2) % 2, r * 2 + v % 2)
                part[spot] = part[spot] + value[r * 128 + v * 8 : r * 128 + v * 8 + 8]
        return carry

    lax.fori_loop(0, 16, phase1, 0)

    def halo(p, carry):
        k = (m + 8 - p) % 8
        block = got.at[k, pl.ds(0, 12)]
        to_above(p, block).wait_recv()
        to_below(p, block).wait_recv()
        second_grads(k)
        return carry

    lax.fori_loop(0, 8, halo, 0)

    def to_pair(q):
        return pltpu.make_async_remote_copy(
            src_ref=part.at[q, 1 - core], dst_ref=paired.at[q],
            send_sem=pair_send.at[q], recv_sem=pair_recv.at[q],
            device_id=device(cx, cy, cz, 1 - core), device_id_type=MESH)

    lax.fori_loop(0, 8, phase2, 0)
    for q in range(4):
        to_pair(q).start()
    lax.fori_loop(8, 16, phase2, 0)

    sources = (None, sum1, sum2)
    landings = (land1, land2, land3)

    def to_owner(q, stage, p):
        axis = ORDERS[q][stage]
        there = (place[axis] + p) % 4
        src = part.at[q, core, there] if stage == 0 else sources[stage].at[q, there]
        return pltpu.make_async_remote_copy(
            src_ref=src, dst_ref=landings[stage].at[q, p - 1],
            send_sem=red_send.at[stage, q, p - 1], recv_sem=red_recv.at[stage, q, p - 1],
            device_id=shifted(axis, p), device_id_type=MESH)

    for q in range(4):
        to_pair(q).wait_recv()
        part[q, core] = part[q, core] + paired[q]
        for p in range(1, 4):
            to_owner(q, 0, p).start()
    for stage in range(3):
        for q in range(4):
            for p in range(1, 4):
                to_owner(q, stage, p).wait_recv()
            mine = place[ORDERS[q][stage]]
            kept = part[q, core, mine] if stage == 0 else sources[stage][q, mine]
            landing = landings[stage]
            value = (kept + landing[q, 0]) + (landing[q, 1] + landing[q, 2])
            if stage == 2:
                out_ref[q // 2, pl.ds((q % 2) * 8, 8), :] = value
            else:
                sources[stage + 1][q] = value
                for p in range(1, 4):
                    to_owner(q, stage + 1, p).start()

    def end_peer(p, carry):
        to_peer(p).wait_send()
        return carry

    def end_halo(p, carry):
        to_above(p, own).wait_send()
        to_below(p, own).wait_send()
        return carry

    lax.fori_loop(1, 8, end_peer, 0)
    lax.fori_loop(0, 8, end_halo, 0)
    for q in range(4):
        to_pair(q).wait_send()
        for stage in range(3):
            for p in range(1, 4):
                to_owner(q, stage, p).wait_send()


def per_device(test_modes, modes):
    def lines(value):
        count = value.shape[0]
        value = value.reshape(count, 3, 8, 2, 2, 128).transpose(0, 1, 2, 4, 3, 5)
        return value.reshape(count * 96, 128)

    dma = pltpu.SemaphoreType.DMA
    return pl.pallas_call(
        kernel,
        out_shape=jax.ShapeDtypeStruct((2, 16, 128), F32),
        in_specs=[pl.BlockSpec(memory_space=pl.ANY)] * 2,
        out_specs=pl.BlockSpec(memory_space=pltpu.VMEM),
        scratch_shapes=[
            pltpu.VMEM((1536, 128), F32),
            pltpu.VMEM((3072, 128), F32),
            pltpu.VMEM((8, TILES, 16, 128), F32),
            pltpu.VMEM((8, TILES, 16, 128), F32),
            pltpu.VMEM((8, 12, 16, 128), F32),
            pltpu.VMEM((8, 12, 16, 128), F32),
            pltpu.VMEM((12, 32, 128), F32),
            pltpu.VMEM((3, 3, 4, 128, 128), F32),
            pltpu.VMEM((1536, 256), BF16),
            pltpu.VMEM((4, 2, 4, 4, 4, 8, 128), F32),
            pltpu.VMEM((4, 4, 4, 4, 8, 128), F32),
            pltpu.VMEM((4, 3, 4, 4, 8, 128), F32),
            pltpu.VMEM((4, 4, 4, 8, 128), F32),
            pltpu.VMEM((4, 3, 4, 8, 128), F32),
            pltpu.VMEM((4, 4, 8, 128), F32),
            pltpu.VMEM((4, 3, 8, 128), F32),
            dma((2,)),
            dma((7,)),
            dma((7,)),
            dma((8,)),
            dma((8,)),
            dma((8,)),
            dma((8,)),
            dma((4,)),
            dma((4,)),
            dma((3, 4, 3)),
            dma((3, 4, 3)),
        ],
        compiler_params=pltpu.CompilerParams(
            collective_id=0, has_side_effects=True, vmem_limit_bytes=48 * 1024 * 1024),
    )(lines(test_modes), lines(modes))


def solution(mesh):
    in_specs = (P(None, None, None, "space", None), P("mode", None, None, "space", None))
    out_specs = P("space", "mode", None)
    return jax.shard_map(
        per_device, mesh=mesh, in_specs=in_specs, out_specs=out_specs, check_vma=False
    )
```

time: 156 us -> 66.8 us (0.43)
  Pallas kernels: 0 us -> 63.4 us
  waiting for transfers between devices: 61.7 us -> 0 us
  matrix products: 28.6 us -> 0 us
  local copies, waits for them, and re-layouts: 23.5 us -> 3.15 us
  between operations: 13.5 us -> 0.01 us
  blocking collectives: 12.1 us -> 0 us
  other arithmetic: 11.7 us -> 0 us
  starting transfers between devices: 3.99 us -> 0 us
    pallas_call x0 -> x1, Pallas kernels: none -> 63.4 us  [per_device(): pl.pallas_call(kernel, out_shape=jax.ShapeDtypeStruct((2, 16, 128), F32),...]
    all_gather x1 -> x0, waiting for transfers between devices: 61.6 us -> none  [per_device(): everything = lax.all_gather(mode_flat, 'mode', axis=0, tiled=True)]
    dot_general x2 -> x0, matrix products: 28.6 us -> none  [add_piece(): jnp.einsum('ikbc,jbc->ikj', weighted, piece_block, precision=lax.Precisio...]
    all_to_all x1 -> x0, blocking collectives: 12.1 us -> none  [sent_and_summed(): lax.all_to_all(parts, axis, split_axis=0, concat_axis=0, tiled=True)]
    div x3 -> x0, other arithmetic: 8.51 us -> none  [the longest x2 4.57 us: central_diff(): return (8.0 * ahead - farther) / 12.0]
    mul x4 -> x0, local copies, waits for them, and re-layouts: 4.42 us -> none  [weigh(): weighted = test_block[:, 0, None, None, :] * grad_block[None, :, 0]]
    concatenate x9 -> x0, local copies, waits for them, and re-layouts: 4.4 us -> none  [the longest x5 2.35 us: central_diff(): ahead = jnp.roll(field, -1, along) - jnp.roll(field, 1, along)]
    reshape x2 -> x0, local copies, waits for them, and re-layouts: 4.01 us -> none  [the longest x1 2.41 us: per_device(): test_flat = test_modes.reshape(test_count, 3, -1)]
  transfers between devices with their start and end apart: 3 -> 0, of which waited for: 1 -> 0; matrix products, arithmetic and copies ran while one was open for 17% -> 0% of each run, Pallas kernels for 0% -> 0%
where the time goes in v1:
time: 66.8 us; the launch traced here: 66.6 us
  Pallas kernels  63.4 us (95%)
  local copies, waits for them, and re-layouts  3.15 us (5%)
    pallas_call x1, Pallas kernels, per_device(): pl.pallas_call(kernel, out_shape=jax.ShapeDtypeStruct((2, 16, 128), F32),...  63.4 us
    unnamed x5, local copies, waits for them, and re-layouts  3.15 us

profile of v1, /device:TPU:0, one launch (start us, length us, event | category | flops | bytes accessed | tf_op | source)
XLA Modules:
  0.0 66.6 jit_solution(15895770362418765940)
XLA Ops:
  0.0 0.0 copy-start
  0.0 1.4 %copy-done = f32[32,3,8,2,256]{4,3,2,1,0:T(2,128)S(1)} copy-done((f32[32,3,8,2,256]{4,3,2,1,0:T(2,128)S(1)}, f32[32,3,8,2,256]{4,3,2,1,0:T(2,128)}, u32[]{:S(2)}) %copy-start) | copy-done | bytes 1572888
  1.4 0.0 copy-start.1
  1.4 1.1 %copy-done.1 = f32[16,3,8,2,256]{4,3,2,1,0:T(2,128)S(1)} copy-done((f32[16,3,8,2,256]{4,3,2,1,0:T(2,128)S(1)}, f32[16,3,8,2,256]{4,3,2,1,0:T(2,128)}, u32[]{:S(2)}) %copy-start.1) | copy-done | bytes 786456
  2.5 63.4 %shard_map.28 = f32[2,16,128]{2,1,0:T(8,128)S(1)} custom-call(f32[3072,128]{1,0:T(8,128)S(1)} %bitcast.10, f32[1536,128]{1,0:T(8,128)S(1)} %bitcast.11), custom_call_target="tpu_custom_call" | custom-call | tf_op jit(solution)/shard_map/pallas_call | solution.py:345
  66.0 0.6 copy.6
Async XLA Ops:
  0.0 1.4 %copy-start = (f32[32,3,8,2,256]{4,3,2,1,0:T(2,128)S(1)}, f32[32,3,8,2,256]{4,3,2,1,0:T(2,128)}, u32[]{:S(2)}) copy-start(f32[32,3,8,2,256]{4,3,2,1,0:T(2,128)} %param.2) | copy-start | bytes 4718596
  1.4 1.1 %copy-start.1 = (f32[16,3,8,2,256]{4,3,2,1,0:T(2,128)S(1)}, f32[16,3,8,2,256]{4,3,2,1,0:T(2,128)}, u32[]{:S(2)}) copy-start(f32[16,3,8,2,256]{4,3,2,1,0:T(2,128)} %param.3) | copy-start | bytes 2359300

commit v2 on v0

v2 whole, which is shorter than its diff:
```python
import jax
import jax.numpy as jnp
from jax import lax
from jax.experimental import pallas as pl
from jax.experimental.pallas import tpu as pltpu
from jax.sharding import PartitionSpec as P

F32 = jnp.float32
BF16 = jnp.bfloat16
MESH = pl.DeviceIdType.MESH
SCALE = 1.0 / 12.0 / 256.0
X, Y, Z = 0, 1, 2
ORDERS = ((X, Y, Z), (Y, Z, X), (Z, X, Y), (Y, X, Z))


def rem(value, size):
    return lax.rem(value, jnp.int32(size)) if isinstance(value, jax.Array) else value % size


def div(value, size):
    return lax.div(value, jnp.int32(size)) if isinstance(value, jax.Array) else value // size


def kernel(test_hbm, mode_hbm, out_ref, x_modes, x_tests, sent, got, up, down, tests, lent,
           grads, rhs, part, paired, land1, sum1, land2, sum2, land3, load_sem, a2a_send, a2a_recv,
           up_send, down_send, up_recv, down_recv, test_send, test_recv, pair_send, pair_recv, red_send, red_recv):
    s = lax.axis_index("space")
    m = lax.axis_index("mode")
    core = rem(s, 2)
    cy = rem(div(s, 2), 4)
    zlo = div(s, 8)
    cx = div(m, 2)
    zhi = rem(m, 2)
    cz = zhi * 2 + zlo
    place = (cx, cy, cz)

    def device(x, y, z, c):
        return (rem(z, 2) * 8 + y * 2 + c, x * 2 + div(z, 2))

    def shifted(axis, step):
        there = list(place)
        there[axis] = rem(there[axis] + step, 4)
        return device(*there, core)

    load_modes = pltpu.make_async_copy(mode_hbm, x_modes, load_sem.at[0])
    load_tests = pltpu.make_async_copy(test_hbm, x_tests, load_sem.at[1])
    load_modes.start()
    load_tests.start()

    barrier = pltpu.get_barrier_semaphore()
    spot = cy * 2 + core

    def ring(step):
        there = rem(spot + step + 8, 8)
        return device(cx, div(there, 2), cz, rem(there, 2))

    def in_plane(n):
        return device(rem(cx + div(n, 4), 4), cy, rem(cz + rem(n, 4), 4), core)

    friends = [in_plane(n) for n in range(1, 16)]
    friends += [ring(1), ring(-1)]
    friends += [shifted(Y, p) for p in range(1, 4)]
    for friend in friends:
        pl.semaphore_signal(barrier, inc=1, device_id=friend, device_id_type=MESH)

    lane = lax.broadcasted_iota(jnp.int32, (8, 128), 1)
    within = lane % 16
    group = lane // 16

    load_modes.wait()

    def arrange(n, carry):
        y, a = div(n, 3), rem(n, 3)
        for xt in range(2):
            for kh in range(2):
                rows = [
                    x_modes[pl.ds(a * 32 + y + kh * 768 + z * 4 + xt * 2, 8, stride=96), :]
                    for z in range(8)
                ]
                for step in (4, 2, 1):
                    low = (group // step) % 2 == 0
                    for z in range(8):
                        if (z // step) % 2 == 0:
                            first, second = rows[z], rows[z + step]
                            rows[z] = jnp.where(low, first, pltpu.roll(second, 16 * step, 1))
                            rows[z + step] = jnp.where(
                                low, pltpu.roll(first, 128 - 16 * step, 1), second)
                for c in range(8):
                    sent[xt * 8 + c, n, pl.ds(kh * 8, 8), :] = rows[c]
        return carry

    lax.fori_loop(0, 6, arrange, 0)

    def edges(d, carry):
        left, right = rem(d + 15, 16), rem(d + 1, 16)
        for y in range(2):
            for kh in range(2):
                rows = pl.ds(kh * 8, 8)
                packed = jnp.zeros((8, 128), F32)
                for slot in range(3):
                    turn = 4 * slot - 14
                    from_left = pltpu.roll(sent[left, y * 3 + slot, rows, :], (turn - 16) % 128, 1)
                    from_right = pltpu.roll(sent[right, y * 3 + slot, rows, :], (turn + 16) % 128, 1)
                    place_in = within - 4 * slot
                    packed = jnp.where((place_in == 0) | (place_in == 1), from_left, packed)
                    packed = jnp.where((place_in == 2) | (place_in == 3), from_right, packed)
                sent[d, 6 + y, rows, :] = packed
        return carry

    lax.fori_loop(0, 16, edges, 0)

    pl.semaphore_wait(barrier, len(friends))

    def source(n):
        x, z = rem(cx + 4 - div(n, 4), 4), rem(cz + 4 - rem(n, 4), 4)
        return rem(z, 2), x * 2 + div(z, 2)

    def to_peer(n):
        column = rem(cx + div(n, 4), 4) * 4 + rem(cz + rem(n, 4), 4)
        return pltpu.make_async_remote_copy(
            src_ref=sent.at[column], dst_ref=got.at[zlo, m],
            send_sem=a2a_send.at[n], recv_sem=a2a_recv.at[n],
            device_id=in_plane(n), device_id_type=MESH)

    def to_above(n, src):
        slab, k = source(n)
        slab = rem(slab + div(spot, 7), 2)
        return pltpu.make_async_remote_copy(
            src_ref=src, dst_ref=down.at[slab, k],
            send_sem=up_send.at[n], recv_sem=down_recv.at[slab * 8 + k],
            device_id=ring(1), device_id_type=MESH)

    def to_below(n, src):
        slab, k = source(n)
        slab = rem(slab + div(7 - spot, 7), 2)
        return pltpu.make_async_remote_copy(
            src_ref=src, dst_ref=up.at[slab, k],
            send_sem=down_send.at[n], recv_sem=up_recv.at[slab * 8 + k],
            device_id=ring(-1), device_id_type=MESH)

    def from_ring(slab, k):
        for buffer, sems, sends in ((down, down_recv, up_send), (up, up_recv, down_send)):
            pltpu.make_async_remote_copy(
                src_ref=got.at[slab, k, pl.ds(0, 6)], dst_ref=buffer.at[slab, k],
                send_sem=sends.at[0], recv_sem=sems.at[slab * 8 + k],
                device_id=ring(1), device_id_type=MESH).wait_recv()

    own = sent.at[cx * 4 + cz, pl.ds(0, 6)]
    for n in range(1, 16):
        to_peer(n).start()
    to_above(0, own).start()
    to_below(0, own).start()

    load_tests.wait()

    def arrange_tests(y):
        c_mine = rem(cx, 2) * 4 + cz
        c_lent = rem(cx, 2) * 4 + rem(cz + (1 if y == 0 else 3), 4)

        def one(a, carry):
            for ih in range(4):
                start = a * 32 + y + div(cx, 2) * 2 + ih * 768
                turned = [
                    pltpu.roll(x_tests[pl.ds(start + z * 4, 8, stride=96), :], 16 * z, 1)
                    if z else x_tests[pl.ds(start, 8, stride=96), :]
                    for z in range(8)
                ]

                def pick(c):
                    value = turned[0]
                    for z in range(1, 8):
                        value = jnp.where((group + 8 - z) % 8 == c, turned[z], value)
                    return pltpu.roll(value, (128 - 16 * c) % 128, 1)

                rows = pl.ds(ih * 8, 8)
                tests[zlo, y, a, rows, :] = pick(c_mine)
                lent[y, a, rows, :] = pick(c_lent)
            return carry

        lax.fori_loop(0, 3, one, 0)

    def to_borrower(y):
        return pltpu.make_async_remote_copy(
            src_ref=lent.at[y], dst_ref=tests.at[zlo, y],
            send_sem=test_send.at[y], recv_sem=test_recv.at[y],
            device_id=shifted(Z, 1 if y == 0 else 3), device_id_type=MESH)

    def wait_tests(y):
        pltpu.make_async_remote_copy(
            src_ref=lent.at[y], dst_ref=tests.at[1 - zlo, y],
            send_sem=test_send.at[y], recv_sem=test_recv.at[y],
            device_id=shifted(Z, 1 if y == 0 else 3), device_id_type=MESH).wait_recv()

    for y in range(2):
        arrange_tests(y)
        to_borrower(y).start()

    def split(value):
        high = value.astype(BF16)
        return high, (value - high.astype(F32)).astype(BF16)

    in16 = lax.broadcasted_iota(jnp.int32, (16, 128), 1) % 16

    def first_grads(n, y):
        slab, k = source(n)
        rows = pl.ds(pl.multiple_of(k * 16, 16), 16)
        packed = got[slab, k, 6 + y]
        for a in range(3):
            f = got[slab, k, y * 3 + a]
            near = pltpu.roll(f, 112, 1) - pltpu.roll(f, 16, 1)
            far = pltpu.roll(f, 96, 1) - pltpu.roll(f, 32, 1)
            grads[2, y, a, slab, rows, :] = (8.0 * near - far) * SCALE

            def at_edge(step, edge):
                moved = pltpu.roll(f, step % 128, 1)
                halo = pltpu.roll(packed, (14 - 4 * a + step) % 128, 1)
                return jnp.where(edge, halo, moved)

            near = at_edge(-1, in16 == 15) - at_edge(1, in16 == 0)
            far = at_edge(-2, in16 >= 14) - at_edge(2, in16 <= 1)
            grads[0, y, a, slab, rows, :] = (8.0 * near - far) * SCALE

    def second_grads(n):
        slab, k = source(n)
        from_ring(slab, k)
        rows = pl.ds(pl.multiple_of(k * 16, 16), 16)
        for a in range(3):
            f0, f1 = got[slab, k, a], got[slab, k, 3 + a]
            f2, f3 = up[slab, k, a], up[slab, k, 3 + a]
            b2, b1 = down[slab, k, a], down[slab, k, 3 + a]
            grads[1, 0, a, slab, rows, :] = (8.0 * (f1 - b1) - (f2 - b2)) * SCALE
            grads[1, 1, a, slab, rows, :] = (8.0 * (f2 - f0) - (f3 - b1)) * SCALE

    def arrival(n):
        slab, k = source(n)
        to_peer(n).wait_recv()
        block = got.at[slab, k, pl.ds(0, 6)]
        to_above(n, block).start()
        to_below(n, block).start()

    def turn_modes(y):
        def turn_tile(n, carry):
            field = got[rem(n, 2), :, y * 3 + div(n, 2)].reshape(128, 128).T
            high, low = split(field)
            rows = pl.ds(pl.multiple_of((div(n, 2) * 4 + y * 2 + rem(n, 2)) * 128, 128), 128)
            rhs[rows, 0:128] = high
            rhs[rows, 128:256] = low
            return carry

        lax.fori_loop(0, 6, turn_tile, 0)

    def triads(c, y, terms):
        total = None
        for b, row in terms:
            columns = []
            for slab in range(2):
                blocks = []
                for zl in range(2):
                    for r in range(2):
                        i = (zl * 8 + y * 2 + c) * 2 + r
                        value = None
                        for a in range(3):
                            line = tests[slab, row, a, pl.ds(i, 1), :]
                            term = line * grads[b, row, a, slab]
                            value = term if value is None else value + term
                        blocks.append(value)
                columns.append(blocks)
            pieces = []
            for n in range(4):
                high, low = split(jnp.concatenate([columns[0][n], columns[1][n]], axis=1))
                pieces += [high, low]
            left = jnp.concatenate(pieces, axis=0)
            right = rhs[(b * 4 + row * 2) * 128 : (b * 4 + row * 2 + 2) * 128, :]
            piece = jnp.dot(left, right, preferred_element_type=F32)
            total = piece if total is None else total + piece
        values = []
        for n in range(4):
            high, low = total[n * 256 : n * 256 + 128], total[n * 256 + 128 : n * 256 + 256]
            values.append((high[:, :128] + high[:, 128:]) + (low[:, :128] + low[:, 128:]))
        return values

    def step(c, y, terms, add):
        values = triads(c, y, terms)
        for n in range(4):
            zl, r = n // 2, n % 2
            for v in range(16):
                spot = (r * 2 + v % 2, c, y, v // 4, zl * 2 + (v // 2) % 2)
                piece = values[n][v * 8 : v * 8 + 8]
                part[spot] = part[spot] + piece if add else piece

    got[zlo, m] = sent[cx * 4 + cz]
    first_grads(0, 0)
    first_grads(0, 1)

    def arrivals(n, carry):
        arrival(n)
        first_grads(n, 0)
        first_grads(n, 1)
        return carry

    lax.fori_loop(1, 16, arrivals, 0)
    for y in range(2):
        turn_modes(y)
        wait_tests(y)

    def phase1(p, carry):
        step(rem(p, 2), div(p, 2), ((0, 0), (2, 0), (0, 1), (2, 1)), False)
        return carry

    lax.fori_loop(0, 8, phase1, 0)

    def halos(n, carry):
        second_grads(n)
        return carry

    lax.fori_loop(0, 16, halos, 0)

    def plane(z):
        return rem(z, 2) * 2 + div(z, 2)

    def spot_of(axis, step):
        there = rem(place[axis] + step, 4)
        return plane(there) if axis == Z else there

    def to_pair(y):
        return pltpu.make_async_remote_copy(
            src_ref=part.at[:, 1 - core, y], dst_ref=paired.at[y],
            send_sem=pair_send.at[y], recv_sem=pair_recv.at[y],
            device_id=device(cx, cy, cz, 1 - core), device_id_type=MESH)

    def first_sum(q, p, y):
        axis = ORDERS[q][0]
        there = spot_of(axis, p)
        if axis == Y:
            src, dst = part.at[q, core, y], land1.at[q, p - 1]
        elif axis == X:
            src, dst = part.at[q, core, y, there], land1.at[q, p - 1, y]
        else:
            src, dst = part.at[q, core, y, :, there], land1.at[q, p - 1, y]
        return pltpu.make_async_remote_copy(
            src_ref=src, dst_ref=dst,
            send_sem=red_send.at[0, q, p - 1], recv_sem=red_recv.at[0, q, p - 1],
            device_id=shifted(axis, p), device_id_type=MESH)

    def first_wait(q, p):
        axis = ORDERS[q][0]
        return pltpu.make_async_remote_copy(
            src_ref=sum1.at[q], dst_ref=land1.at[q, p - 1],
            send_sem=red_send.at[0, q, p - 1], recv_sem=red_recv.at[0, q, p - 1],
            device_id=shifted(axis, p), device_id_type=MESH)

    def finish_group(g):
        y = rem(cy + g + 1, 4)
        to_pair(y).wait_recv()
        for q in range(4):
            part[q, core, y] = part[q, core, y] + paired[y, q]
        for q in range(4):
            if ORDERS[q][0] == Y:
                if g < 3:
                    first_sum(q, g + 1, y).start()
            else:
                for p in range(1, 4):
                    first_sum(q, p, y).start()

    for g in range(4):
        y = rem(cy + g + 1, 4)

        def phase3(h, carry):
            c = jnp.where(h == 0, 1 - core, core)
            step(c, y, ((1, 0), (1, 1)), True)

            @pl.when(h == 0)
            def _():
                to_pair(y).start()

            return carry

        lax.fori_loop(0, 2, phase3, 0)
        if g > 0:
            finish_group(g - 1)
    finish_group(3)

    def dims_after(q):
        return [axis for axis in (Y, X, Z) if axis != ORDERS[q][0]]

    def second_sum(q, p):
        axis = ORDERS[q][1]
        there = spot_of(axis, p)
        src = sum1.at[q, there] if dims_after(q)[0] == axis else sum1.at[q, :, there]
        return pltpu.make_async_remote_copy(
            src_ref=src, dst_ref=land2.at[q, p - 1],
            send_sem=red_send.at[1, q, p - 1], recv_sem=red_recv.at[1, q, p - 1],
            device_id=shifted(axis, p), device_id_type=MESH)

    def third_sum(q, p):
        axis = ORDERS[q][2]
        return pltpu.make_async_remote_copy(
            src_ref=sum2.at[q, spot_of(axis, p)], dst_ref=land3.at[q, p - 1],
            send_sem=red_send.at[2, q, p - 1], recv_sem=red_recv.at[2, q, p - 1],
            device_id=shifted(axis, p), device_id_type=MESH)

    def added(kept, landing):
        return (kept + landing[0]) + (landing[1] + landing[2])

    for q in range(4):
        for p in range(1, 4):
            first_wait(q, p).wait_recv()
        axis = ORDERS[q][0]
        mine = spot_of(axis, 0)
        if axis == Y:
            kept = part[q, core, mine]
        elif axis == X:
            kept = part[q, core, :, mine]
        else:
            kept = part[q, core, :, :, mine]
        sum1[q] = added(kept, [land1[q, n] for n in range(3)])
        for p in range(1, 4):
            second_sum(q, p).start()
    for q in range(4):
        for p in range(1, 4):
            second_sum(q, p).wait_recv()
        axis = ORDERS[q][1]
        mine = spot_of(axis, 0)
        kept = sum1[q, mine] if dims_after(q)[0] == axis else sum1[q, :, mine]
        sum2[q] = added(kept, [land2[q, n] for n in range(3)])
        for p in range(1, 4):
            third_sum(q, p).start()
    for q in range(4):
        for p in range(1, 4):
            third_sum(q, p).wait_recv()
        kept = sum2[q, spot_of(ORDERS[q][2], 0)]
        value = added(kept, [land3[q, n] for n in range(3)])
        out_ref[q // 2, pl.ds((q % 2) * 8, 8), :] = value

    for n in range(1, 16):
        to_peer(n).wait_send()
    for n in range(16):
        to_above(n, own).wait_send()
        to_below(n, own).wait_send()
    for y in range(2):
        to_borrower(y).wait_send()
    for y in range(4):
        to_pair(y).wait_send()
    for q in range(4):
        for p in range(1, 4):
            first_wait(q, p).wait_send()
            second_sum(q, p).wait_send()
            third_sum(q, p).wait_send()


def per_device(test_modes, modes):
    def lines(value):
        count = value.shape[0]
        value = value.reshape(count, 3, 8, 2, 2, 128).transpose(0, 1, 2, 4, 3, 5)
        return value.reshape(count * 96, 128)

    dma = pltpu.SemaphoreType.DMA
    return pl.pallas_call(
        kernel,
        out_shape=jax.ShapeDtypeStruct((2, 16, 128), F32),
        in_specs=[pl.BlockSpec(memory_space=pltpu.HBM)] * 2,
        out_specs=pl.BlockSpec(memory_space=pltpu.VMEM),
        scratch_shapes=[
            pltpu.VMEM((1536, 128), F32),
            pltpu.VMEM((3072, 128), F32),
            pltpu.VMEM((16, 8, 16, 128), F32),
            pltpu.VMEM((2, 8, 8, 16, 128), F32),
            pltpu.VMEM((2, 8, 6, 16, 128), F32),
            pltpu.VMEM((2, 8, 6, 16, 128), F32),
            pltpu.VMEM((2, 2, 3, 32, 128), F32),
            pltpu.VMEM((2, 3, 32, 128), F32),
            pltpu.VMEM((3, 2, 3, 2, 128, 128), F32),
            pltpu.VMEM((1536, 256), BF16),
            pltpu.VMEM((4, 2, 4, 4, 4, 8, 128), F32),
            pltpu.VMEM((4, 4, 4, 4, 8, 128), F32),
            pltpu.VMEM((4, 3, 4, 4, 8, 128), F32),
            pltpu.VMEM((4, 4, 4, 8, 128), F32),
            pltpu.VMEM((4, 3, 4, 8, 128), F32),
            pltpu.VMEM((4, 4, 8, 128), F32),
            pltpu.VMEM((4, 3, 8, 128), F32),
            dma((2,)),
            dma((16,)),
            dma((16,)),
            dma((16,)),
            dma((16,)),
            dma((16,)),
            dma((16,)),
            dma((2,)),
            dma((2,)),
            dma((4,)),
            dma((4,)),
            dma((3, 4, 3)),
            dma((3, 4, 3)),
        ],
        compiler_params=pltpu.CompilerParams(
            collective_id=0, has_side_effects=True, vmem_limit_bytes=62 * 1024 * 1024),
    )(lines(test_modes), lines(modes))


def solution(mesh):
    in_specs = (P(None, None, None, "space", None), P("mode", None, None, "space", None))
    out_specs = P("space", "mode", None)
    return jax.shard_map(
        per_device, mesh=mesh, in_specs=in_specs, out_specs=out_specs, check_vma=False
    )
```

time: 156 us -> 59.5 us (0.38)
  waiting for transfers between devices: 61.7 us -> 0 us
  Pallas kernels: 0 us -> 58 us
  matrix products: 28.6 us -> 0 us
  local copies, waits for them, and re-layouts: 23.5 us -> 1.32 us
  between operations: 13.5 us -> 0.01 us
  blocking collectives: 12.1 us -> 0 us
  other arithmetic: 11.7 us -> 0 us
  starting transfers between devices: 3.99 us -> 0 us
    all_gather x1 -> x0, waiting for transfers between devices: 61.6 us -> none  [per_device(): everything = lax.all_gather(mode_flat, 'mode', axis=0, tiled=True)]
    pallas_call x0 -> x1, Pallas kernels: none -> 58 us  [per_device(): pl.pallas_call(kernel, out_shape=jax.ShapeDtypeStruct((2, 16, 128), F32),...]
    dot_general x2 -> x0, matrix products: 28.6 us -> none  [add_piece(): jnp.einsum('ikbc,jbc->ikj', weighted, piece_block, precision=lax.Precisio...]
    all_to_all x1 -> x0, blocking collectives: 12.1 us -> none  [sent_and_summed(): lax.all_to_all(parts, axis, split_axis=0, concat_axis=0, tiled=True)]
    div x3 -> x0, other arithmetic: 8.51 us -> none  [the longest x2 4.57 us: central_diff(): return (8.0 * ahead - farther) / 12.0]
    mul x4 -> x0, local copies, waits for them, and re-layouts: 4.42 us -> none  [weigh(): weighted = test_block[:, 0, None, None, :] * grad_block[None, :, 0]]
    concatenate x9 -> x0, local copies, waits for them, and re-layouts: 4.4 us -> none  [the longest x5 2.35 us: central_diff(): ahead = jnp.roll(field, -1, along) - jnp.roll(field, 1, along)]
    reshape x2 -> x0, local copies, waits for them, and re-layouts: 4.01 us -> none  [the longest x1 2.41 us: per_device(): test_flat = test_modes.reshape(test_count, 3, -1)]
  transfers between devices with their start and end apart: 3 -> 0, of which waited for: 1 -> 0; matrix products, arithmetic and copies ran while one was open for 17% -> 0% of each run, Pallas kernels for 0% -> 0%
where the time goes in v2:
time: 59.5 us; the launch traced here: 59.3 us
  Pallas kernels  58 us (97%)
  local copies, waits for them, and re-layouts  1.32 us (2%)
    pallas_call x1, Pallas kernels, per_device(): pl.pallas_call(kernel, out_shape=jax.ShapeDtypeStruct((2, 16, 128), F32),...  58 us
    unnamed x1, local copies, waits for them, and re-layouts  1.32 us

profile of v2, /device:TPU:0, one launch (start us, length us, event | category | flops | bytes accessed | tf_op | source)
XLA Modules:
  0.0 59.3 jit_solution(18275755091930212799)
XLA Ops:
  0.0 58.0 %shard_map.28 = f32[2,16,128]{2,1,0:T(8,128)} custom-call(f32[3072,128]{1,0:T(8,128)} %bitcast.10, f32[1536,128]{1,0:T(8,128)} %bitcast.11), custom_call_target="tpu_custom_call" | custom-call | tf_op jit(solution)/shard_map/pallas_call | solution.py:458
  58.0 1.3 %copy.6 = f32[2,16,128]{2,1,0:T(8,128)} copy(f32[2,16,128]{2,1,0:T(8,128)} %shard_map.28) | data formatting | bytes 32768

commit v3 on v2

--- a/solution.py
+++ b/solution.py
@@ -10,6 +10,7 @@
 MESH = pl.DeviceIdType.MESH
 SCALE = 1.0 / 12.0 / 256.0
 X, Y, Z = 0, 1, 2
+PEERS = (10, 6, 14, 9, 11, 5, 15, 7, 13, 8, 2, 4, 1, 12, 3)
 ORDERS = ((X, Y, Z), (Y, Z, X), (Z, X, Y), (Y, X, Z))
 
 
@@ -86,25 +87,25 @@
                             rows[z + step] = jnp.where(
                                 low, pltpu.roll(first, 128 - 16 * step, 1), second)
                 for c in range(8):
-                    sent[xt * 8 + c, n, pl.ds(kh * 8, 8), :] = rows[c]
+                    sent[xt * 8 + c, pl.ds(n * 16 + kh * 8, 8), :] = rows[c]
         return carry
 
     lax.fori_loop(0, 6, arrange, 0)
 
     def edges(d, carry):
         left, right = rem(d + 15, 16), rem(d + 1, 16)
-        for y in range(2):
-            for kh in range(2):
-                rows = pl.ds(kh * 8, 8)
-                packed = jnp.zeros((8, 128), F32)
-                for slot in range(3):
-                    turn = 4 * slot - 14
-                    from_left = pltpu.roll(sent[left, y * 3 + slot, rows, :], (turn - 16) % 128, 1)
-                    from_right = pltpu.roll(sent[right, y * 3 + slot, rows, :], (turn + 16) % 128, 1)
-                    place_in = within - 4 * slot
-                    packed = jnp.where((place_in == 0) | (place_in == 1), from_left, packed)
-                    packed = jnp.where((place_in == 2) | (place_in == 3), from_right, packed)
-                sent[d, 6 + y, rows, :] = packed
+        for n in range(3):
+            packed = jnp.zeros((8, 128), F32)
+            for slot in range(4):
+                kh, tile = (4 * n + slot) // 6, (4 * n + slot) % 6
+                rows = pl.ds(tile * 16 + kh * 8, 8)
+                turn = 4 * slot - 14
+                from_left = pltpu.roll(sent[left, rows, :], (turn - 16) % 128, 1)
+                from_right = pltpu.roll(sent[right, rows, :], (turn + 16) % 128, 1)
+                place_in = within - 4 * slot
+                packed = jnp.where((place_in == 0) | (place_in == 1), from_left, packed)
+                packed = jnp.where((place_in == 2) | (place_in == 3), from_right, packed)
+            sent[d, pl.ds(96 + n * 8, 8), :] = packed
         return carry
 
     lax.fori_loop(0, 16, edges, 0)
@@ -141,12 +142,12 @@
     def from_ring(slab, k):
         for buffer, sems, sends in ((down, down_recv, up_send), (up, up_recv, down_send)):
             pltpu.make_async_remote_copy(
-                src_ref=got.at[slab, k, pl.ds(0, 6)], dst_ref=buffer.at[slab, k],
+                src_ref=got.at[slab, k, pl.ds(0, 96)], dst_ref=buffer.at[slab, k],
                 send_sem=sends.at[0], recv_sem=sems.at[slab * 8 + k],
                 device_id=ring(1), device_id_type=MESH).wait_recv()
 
-    own = sent.at[cx * 4 + cz, pl.ds(0, 6)]
-    for n in range(1, 16):
+    own = sent.at[cx * 4 + cz, pl.ds(0, 96)]
+    for n in PEERS:
         to_peer(n).start()
     to_above(0, own).start()
     to_below(0, own).start()
@@ -199,48 +200,50 @@
         high = value.astype(BF16)
         return high, (value - high.astype(F32)).astype(BF16)
 
-    in16 = lax.broadcasted_iota(jnp.int32, (16, 128), 1) % 16
-
-    def first_grads(n, y):
+    def first_grads(n):
         slab, k = source(n)
-        rows = pl.ds(pl.multiple_of(k * 16, 16), 16)
-        packed = got[slab, k, 6 + y]
-        for a in range(3):
-            f = got[slab, k, y * 3 + a]
-            near = pltpu.roll(f, 112, 1) - pltpu.roll(f, 16, 1)
-            far = pltpu.roll(f, 96, 1) - pltpu.roll(f, 32, 1)
-            grads[2, y, a, slab, rows, :] = (8.0 * near - far) * SCALE
-
-            def at_edge(step, edge):
-                moved = pltpu.roll(f, step % 128, 1)
-                halo = pltpu.roll(packed, (14 - 4 * a + step) % 128, 1)
-                return jnp.where(edge, halo, moved)
-
-            near = at_edge(-1, in16 == 15) - at_edge(1, in16 == 0)
-            far = at_edge(-2, in16 >= 14) - at_edge(2, in16 <= 1)
-            grads[0, y, a, slab, rows, :] = (8.0 * near - far) * SCALE
+        for tile in range(6):
+            for kh in range(2):
+                y, a = tile // 3, tile % 3
+                rows = pl.ds(pl.multiple_of(k * 16 + kh * 8, 8), 8)
+                f = got[slab, k, tile * 16 + kh * 8 : tile * 16 + kh * 8 + 8]
+                near = pltpu.roll(f, 112, 1) - pltpu.roll(f, 16, 1)
+                far = pltpu.roll(f, 96, 1) - pltpu.roll(f, 32, 1)
+                grads[2, y, a, slab, rows, :] = (8.0 * near - far) * SCALE
+                item = kh * 6 + tile
+                packed = got[slab, k, 96 + item // 4 * 8 : 104 + item // 4 * 8]
+
+                def at_edge(step, edge):
+                    moved = pltpu.roll(f, step % 128, 1)
+                    halo = pltpu.roll(packed, (14 - 4 * (item % 4) + step) % 128, 1)
+                    return jnp.where(edge, halo, moved)
+
+                near = at_edge(-1, within == 15) - at_edge(1, within == 0)
+                far = at_edge(-2, within >= 14) - at_edge(2, within <= 1)
+                grads[0, y, a, slab, rows, :] = (8.0 * near - far) * SCALE
 
     def second_grads(n):
         slab, k = source(n)
         from_ring(slab, k)
         rows = pl.ds(pl.multiple_of(k * 16, 16), 16)
         for a in range(3):
-            f0, f1 = got[slab, k, a], got[slab, k, 3 + a]
-            f2, f3 = up[slab, k, a], up[slab, k, 3 + a]
-            b2, b1 = down[slab, k, a], down[slab, k, 3 + a]
+            f0, f1 = got[slab, k, a * 16 : a * 16 + 16], got[slab, k, a * 16 + 48 : a * 16 + 64]
+            f2, f3 = up[slab, k, a * 16 : a * 16 + 16], up[slab, k, a * 16 + 48 : a * 16 + 64]
+            b2, b1 = down[slab, k, a * 16 : a * 16 + 16], down[slab, k, a * 16 + 48 : a * 16 + 64]
             grads[1, 0, a, slab, rows, :] = (8.0 * (f1 - b1) - (f2 - b2)) * SCALE
             grads[1, 1, a, slab, rows, :] = (8.0 * (f2 - f0) - (f3 - b1)) * SCALE
 
     def arrival(n):
         slab, k = source(n)
         to_peer(n).wait_recv()
-        block = got.at[slab, k, pl.ds(0, 6)]
+        block = got.at[slab, k, pl.ds(0, 96)]
         to_above(n, block).start()
         to_below(n, block).start()
 
     def turn_modes(y):
         def turn_tile(n, carry):
-            field = got[rem(n, 2), :, y * 3 + div(n, 2)].reshape(128, 128).T
+            tile = pl.ds(pl.multiple_of((y * 3 + div(n, 2)) * 16, 16), 16)
+            field = got[rem(n, 2), :, tile, :].reshape(128, 128).T
             high, low = split(field)
             rows = pl.ds(pl.multiple_of((div(n, 2) * 4 + y * 2 + rem(n, 2)) * 128, 128), 128)
             rhs[rows, 0:128] = high
@@ -250,32 +253,25 @@
         lax.fori_loop(0, 6, turn_tile, 0)
 
     def triads(c, y, terms):
-        total = None
-        for b, row in terms:
-            columns = []
-            for slab in range(2):
-                blocks = []
-                for zl in range(2):
-                    for r in range(2):
-                        i = (zl * 8 + y * 2 + c) * 2 + r
-                        value = None
-                        for a in range(3):
-                            line = tests[slab, row, a, pl.ds(i, 1), :]
-                            term = line * grads[b, row, a, slab]
-                            value = term if value is None else value + term
-                        blocks.append(value)
-                columns.append(blocks)
-            pieces = []
-            for n in range(4):
-                high, low = split(jnp.concatenate([columns[0][n], columns[1][n]], axis=1))
-                pieces += [high, low]
-            left = jnp.concatenate(pieces, axis=0)
-            right = rhs[(b * 4 + row * 2) * 128 : (b * 4 + row * 2 + 2) * 128, :]
-            piece = jnp.dot(left, right, preferred_element_type=F32)
-            total = piece if total is None else total + piece
         values = []
         for n in range(4):
-            high, low = total[n * 256 : n * 256 + 128], total[n * 256 + 128 : n * 256 + 256]
+            zl, r = n // 2, n % 2
+            i = (zl * 8 + y * 2 + c) * 2 + r
+            total = None
+            for b, row in terms:
+                columns = []
+                for slab in range(2):
+                    value = None
+                    for a in range(3):
+                        line = tests[slab, row, a, pl.ds(i, 1), :]
+                        term = line * grads[b, row, a, slab]
+                        value = term if value is None else value + term
+                    columns.append(value)
+                right = rhs[(b * 4 + row * 2) * 128 : (b * 4 + row * 2 + 2) * 128, :]
+                high, low = split(jnp.concatenate(columns, axis=1))
+                piece = jnp.dot(jnp.concatenate([high, low], axis=0), right, preferred_element_type=F32)
+                total = piece if total is None else total + piece
+            high, low = total[:128], total[128:]
             values.append((high[:, :128] + high[:, 128:]) + (low[:, :128] + low[:, 128:]))
         return values
 
@@ -289,16 +285,10 @@
                 part[spot] = part[spot] + piece if add else piece
 
     got[zlo, m] = sent[cx * 4 + cz]
-    first_grads(0, 0)
-    first_grads(0, 1)
-
-    def arrivals(n, carry):
+    first_grads(0)
+    for n in PEERS:
         arrival(n)
-        first_grads(n, 0)
-        first_grads(n, 1)
-        return carry
-
-    lax.fori_loop(1, 16, arrivals, 0)
+        first_grads(n)
     for y in range(2):
         turn_modes(y)
         wait_tests(y)
@@ -432,7 +422,7 @@
         value = added(kept, [land3[q, n] for n in range(3)])
         out_ref[q // 2, pl.ds((q % 2) * 8, 8), :] = value
 
-    for n in range(1, 16):
+    for n in PEERS:
         to_peer(n).wait_send()
     for n in range(16):
         to_above(n, own).wait_send()
@@ -463,10 +453,10 @@
         scratch_shapes=[
             pltpu.VMEM((1536, 128), F32),
             pltpu.VMEM((3072, 128), F32),
-            pltpu.VMEM((16, 8, 16, 128), F32),
-            pltpu.VMEM((2, 8, 8, 16, 128), F32),
-            pltpu.VMEM((2, 8, 6, 16, 128), F32),
-            pltpu.VMEM((2, 8, 6, 16, 128), F32),
+            pltpu.VMEM((16, 120, 128), F32),
+            pltpu.VMEM((2, 8, 120, 128), F32),
+            pltpu.VMEM((2, 8, 96, 128), F32),
+            pltpu.VMEM((2, 8, 96, 128), F32),
             pltpu.VMEM((2, 2, 3, 32, 128), F32),
             pltpu.VMEM((2, 3, 32, 128), F32),
             pltpu.VMEM((3, 2, 3, 2, 128, 128), F32),

time: 59.5 us -> 54.6 us (0.918)
  Pallas kernels: 58 us -> 53.1 us
    pallas_call x1, Pallas kernels: 58 us -> 53.1 us  [per_device(): pl.pallas_call(kernel, out_shape=jax.ShapeDtypeStruct((2, 16, 128), F32),...]
where the time goes in v3:
time: 54.6 us; the launch traced here: 54.5 us
  Pallas kernels  53.1 us (97%)
  local copies, waits for them, and re-layouts  1.32 us (2%)
    pallas_call x1, Pallas kernels, per_device(): pl.pallas_call(kernel, out_shape=jax.ShapeDtypeStruct((2, 16, 128), F32),...  53.1 us
    unnamed x1, local copies, waits for them, and re-layouts  1.32 us

profile of v3, /device:TPU:0, one launch (start us, length us, event | category | flops | bytes accessed | tf_op | source)
XLA Modules:
  0.0 54.5 jit_solution(5189192708263152450)
XLA Ops:
  0.0 53.1 %shard_map.28 = f32[2,16,128]{2,1,0:T(8,128)} custom-call(f32[3072,128]{1,0:T(8,128)} %bitcast.10, f32[1536,128]{1,0:T(8,128)} %bitcast.11), custom_call_target="tpu_custom_call" | custom-call | tf_op jit(solution)/shard_map/pallas_call | solution.py:448
  53.1 1.3 %copy.6 = f32[2,16,128]{2,1,0:T(8,128)} copy(f32[2,16,128]{2,1,0:T(8,128)} %shard_map.28) | data formatting | bytes 32768

commit v4 on v3

--- a/solution.py
+++ b/solution.py
@@ -10,8 +10,10 @@
 MESH = pl.DeviceIdType.MESH
 SCALE = 1.0 / 12.0 / 256.0
 X, Y, Z = 0, 1, 2
+ARRIVAL = (0, 2, 1, 3)
+STEPS = (2, 1, 3)
 PEERS = (10, 6, 14, 9, 11, 5, 15, 7, 13, 8, 2, 4, 1, 12, 3)
-ORDERS = ((X, Y, Z), (Y, Z, X), (Z, X, Y), (Y, X, Z))
+ORDERS = ((X, Y, Z), (Y, Z, X), (Z, X, Y), (Z, Y, X))
 
 
 def rem(value, size):
@@ -213,13 +215,13 @@
                 item = kh * 6 + tile
                 packed = got[slab, k, 96 + item // 4 * 8 : 104 + item // 4 * 8]
 
-                def at_edge(step, edge):
-                    moved = pltpu.roll(f, step % 128, 1)
-                    halo = pltpu.roll(packed, (14 - 4 * (item % 4) + step) % 128, 1)
-                    return jnp.where(edge, halo, moved)
-
-                near = at_edge(-1, within == 15) - at_edge(1, within == 0)
-                far = at_edge(-2, within >= 14) - at_edge(2, within <= 1)
+                edge = pltpu.roll(packed, (14 - 4 * (item % 4)) % 128, 1)
+
+                def moved(step, at_edge):
+                    return pltpu.roll(jnp.where(at_edge, edge, f), step % 128, 1)
+
+                near = moved(-1, within == 0) - moved(1, within == 15)
+                far = moved(-2, within <= 1) - moved(2, within >= 14)
                 grads[0, y, a, slab, rows, :] = (8.0 * near - far) * SCALE
 
     def second_grads(n):
@@ -240,17 +242,18 @@
         to_above(n, block).start()
         to_below(n, block).start()
 
-    def turn_modes(y):
+    def turn_modes(b):
         def turn_tile(n, carry):
-            tile = pl.ds(pl.multiple_of((y * 3 + div(n, 2)) * 16, 16), 16)
-            field = got[rem(n, 2), :, tile, :].reshape(128, 128).T
+            y, slab = div(n, 2), rem(n, 2)
+            tile = pl.ds(pl.multiple_of((y * 3 + b) * 16, 16), 16)
+            field = got[slab, :, tile, :].reshape(128, 128).T
             high, low = split(field)
-            rows = pl.ds(pl.multiple_of((div(n, 2) * 4 + y * 2 + rem(n, 2)) * 128, 128), 128)
+            rows = pl.ds(pl.multiple_of((b * 4 + n) * 128, 128), 128)
             rhs[rows, 0:128] = high
             rhs[rows, 128:256] = low
             return carry
 
-        lax.fori_loop(0, 6, turn_tile, 0)
+        lax.fori_loop(0, 4, turn_tile, 0)
 
     def triads(c, y, terms):
         values = []
@@ -289,8 +292,9 @@
     for n in PEERS:
         arrival(n)
         first_grads(n)
+    turn_modes(0)
+    turn_modes(2)
     for y in range(2):
-        turn_modes(y)
         wait_tests(y)
 
     def phase1(p, carry):
@@ -298,6 +302,7 @@
         return carry
 
     lax.fori_loop(0, 8, phase1, 0)
+    turn_modes(1)
 
     def halos(n, carry):
         second_grads(n)
@@ -349,26 +354,17 @@
                 if g < 3:
                     first_sum(q, g + 1, y).start()
             else:
-                for p in range(1, 4):
+                for p in STEPS:
                     first_sum(q, p, y).start()
 
-    for g in range(4):
+    for g, mine in ((0, False), (1, False), (0, True), (2, False), (1, True), (3, False),
+                    (2, True), (3, True)):
         y = rem(cy + g + 1, 4)
-
-        def phase3(h, carry):
-            c = jnp.where(h == 0, 1 - core, core)
-            step(c, y, ((1, 0), (1, 1)), True)
-
-            @pl.when(h == 0)
-            def _():
-                to_pair(y).start()
-
-            return carry
-
-        lax.fori_loop(0, 2, phase3, 0)
-        if g > 0:
-            finish_group(g - 1)
-    finish_group(3)
+        step(core if mine else 1 - core, y, ((1, 0), (1, 1)), True)
+        if mine:
+            finish_group(g)
+        else:
+            to_pair(y).start()
 
     def dims_after(q):
         return [axis for axis in (Y, X, Z) if axis != ORDERS[q][0]]
@@ -392,7 +388,7 @@
     def added(kept, landing):
         return (kept + landing[0]) + (landing[1] + landing[2])
 
-    for q in range(4):
+    for q in ARRIVAL:
         for p in range(1, 4):
             first_wait(q, p).wait_recv()
         axis = ORDERS[q][0]
@@ -404,18 +400,18 @@
         else:
             kept = part[q, core, :, :, mine]
         sum1[q] = added(kept, [land1[q, n] for n in range(3)])
-        for p in range(1, 4):
+        for p in STEPS:
             second_sum(q, p).start()
-    for q in range(4):
+    for q in ARRIVAL:
         for p in range(1, 4):
             second_sum(q, p).wait_recv()
         axis = ORDERS[q][1]
         mine = spot_of(axis, 0)
         kept = sum1[q, mine] if dims_after(q)[0] == axis else sum1[q, :, mine]
         sum2[q] = added(kept, [land2[q, n] for n in range(3)])
-        for p in range(1, 4):
+        for p in STEPS:
             third_sum(q, p).start()
-    for q in range(4):
+    for q in ARRIVAL:
         for p in range(1, 4):
             third_sum(q, p).wait_recv()
         kept = sum2[q, spot_of(ORDERS[q][2], 0)]

time: 54.6 us -> 53.5 us (0.980)
  Pallas kernels: 53.1 us -> 52 us
    pallas_call x1, Pallas kernels: 53.1 us -> 52 us  [per_device(): pl.pallas_call(kernel, out_shape=jax.ShapeDtypeStruct((2, 16, 128), F32),...]
where the time goes in v4:
time: 53.5 us; the launch traced here: 53.3 us
  Pallas kernels  52 us (97%)
  local copies, waits for them, and re-layouts  1.32 us (2%)
    pallas_call x1, Pallas kernels, per_device(): pl.pallas_call(kernel, out_shape=jax.ShapeDtypeStruct((2, 16, 128), F32),...  52 us
    unnamed x1, local copies, waits for them, and re-layouts  1.32 us

profile of v4, /device:TPU:0, one launch (start us, length us, event | category | flops | bytes accessed | tf_op | source)
XLA Modules:
  0.0 53.3 jit_solution(5961386996776352510)
XLA Ops:
  0.0 52.0 %shard_map.28 = f32[2,16,128]{2,1,0:T(8,128)} custom-call(f32[3072,128]{1,0:T(8,128)} %bitcast.10, f32[1536,128]{1,0:T(8,128)} %bitcast.11), custom_call_target="tpu_custom_call" | custom-call | tf_op jit(solution)/shard_map/pallas_call | solution.py:444
  52.0 1.3 %copy.6 = f32[2,16,128]{2,1,0:T(8,128)} copy(f32[2,16,128]{2,1,0:T(8,128)} %shard_map.28) | data formatting | bytes 32768

commit v5 on v4

--- a/solution.py
+++ b/solution.py
@@ -297,18 +297,16 @@
     for y in range(2):
         wait_tests(y)
 
-    def phase1(p, carry):
-        step(rem(p, 2), div(p, 2), ((0, 0), (2, 0), (0, 1), (2, 1)), False)
+    def phase1(y, carry):
+        for c in range(2):
+            step(c, y, ((0, 0), (2, 0), (0, 1), (2, 1)), False)
         return carry
 
-    lax.fori_loop(0, 8, phase1, 0)
+    lax.fori_loop(0, 4, phase1, 0)
     turn_modes(1)
 
-    def halos(n, carry):
+    for n in (0,) + PEERS:
         second_grads(n)
-        return carry
-
-    lax.fori_loop(0, 16, halos, 0)
 
     def plane(z):
         return rem(z, 2) * 2 + div(z, 2)

time: 53.5 us -> 52.7 us (0.985)
  Pallas kernels: 52 us -> 51.2 us
    pallas_call x1, Pallas kernels: 52 us -> 51.2 us  [per_device(): pl.pallas_call(kernel, out_shape=jax.ShapeDtypeStruct((2, 16, 128), F32),...]
where the time goes in v5:
time: 52.7 us; the launch traced here: 52.5 us
  Pallas kernels  51.2 us (97%)
  local copies, waits for them, and re-layouts  1.32 us (3%)
    pallas_call x1, Pallas kernels, per_device(): pl.pallas_call(kernel, out_shape=jax.ShapeDtypeStruct((2, 16, 128), F32),...  51.2 us
    unnamed x1, local copies, waits for them, and re-layouts  1.32 us

profile of v5, /device:TPU:0, one launch (start us, length us, event | category | flops | bytes accessed | tf_op | source)
XLA Modules:
  0.0 52.5 jit_solution(16668849407680249093)
XLA Ops:
  0.0 51.2 %shard_map.28 = f32[2,16,128]{2,1,0:T(8,128)} custom-call(f32[3072,128]{1,0:T(8,128)} %bitcast.10, f32[1536,128]{1,0:T(8,128)} %bitcast.11), custom_call_target="tpu_custom_call" | custom-call | tf_op jit(solution)/shard_map/pallas_call | solution.py:442
  51.2 1.3 %copy.6 = f32[2,16,128]{2,1,0:T(8,128)} copy(f32[2,16,128]{2,1,0:T(8,128)} %shard_map.28) | data formatting | bytes 32768

commit v6 on v5

--- a/solution.py
+++ b/solution.py
@@ -243,17 +243,14 @@
         to_below(n, block).start()
 
     def turn_modes(b):
-        def turn_tile(n, carry):
-            y, slab = div(n, 2), rem(n, 2)
-            tile = pl.ds(pl.multiple_of((y * 3 + b) * 16, 16), 16)
-            field = got[slab, :, tile, :].reshape(128, 128).T
-            high, low = split(field)
-            rows = pl.ds(pl.multiple_of((b * 4 + n) * 128, 128), 128)
-            rhs[rows, 0:128] = high
-            rhs[rows, 128:256] = low
-            return carry
-
-        lax.fori_loop(0, 4, turn_tile, 0)
+        for y in range(2):
+            for slab in range(2):
+                tile = (y * 3 + b) * 16
+                field = got[slab, :, tile : tile + 16, :].reshape(128, 128).T
+                high, low = split(field)
+                row = (b * 4 + y * 2 + slab) * 128
+                rhs[row : row + 128, 0:128] = high
+                rhs[row : row + 128, 128:256] = low
 
     def triads(c, y, terms):
         values = []

time: 52.7 us -> 52.2 us (level)
  no operation moved by 1% of the time
where the time goes in v6:
time: 52.2 us; the launch traced here: 52 us
  Pallas kernels  50.7 us (97%)
  local copies, waits for them, and re-layouts  1.32 us (3%)
    pallas_call x1, Pallas kernels, per_device(): pl.pallas_call(kernel, out_shape=jax.ShapeDtypeStruct((2, 16, 128), F32),...  50.7 us
    unnamed x1, local copies, waits for them, and re-layouts  1.32 us

profile of v6, /device:TPU:0, one launch (start us, length us, event | category | flops | bytes accessed | tf_op | source)
XLA Modules:
  0.0 52.0 jit_solution(1473576899870459032)
XLA Ops:
  0.0 50.7 %shard_map.28 = f32[2,16,128]{2,1,0:T(8,128)} custom-call(f32[3072,128]{1,0:T(8,128)} %bitcast.10, f32[1536,128]{1,0:T(8,128)} %bitcast.11), custom_call_target="tpu_custom_call" | custom-call | tf_op jit(solution)/shard_map/pallas_call | solution.py:439
  50.7 1.3 %copy.6 = f32[2,16,128]{2,1,0:T(8,128)} copy(f32[2,16,128]{2,1,0:T(8,128)} %shard_map.28) | data formatting | bytes 32768
